TPU v7x, 256 devices: a whole 4x4x8 slice. The times are simulated.
256 devices in a mesh: bra: 16 (over z_lo, x), ket: 8 (over y, core), mpo: 2 (over z_hi).
Axes of the slice: x: 4, y: 4, z: 8 (z_hi: 2, z_lo: 4; z = z_hi * 4 + z_lo), core: 2. Of those that a mesh axis runs over, the one named last changes fastest.
Arguments:
- left_env: bfloat16 [4, 3072, 3072], P('mpo', 'bra', 'ket'), may hold values from -6 to 6
- site_tensor: bfloat16 [3072, 4, 3072], P('bra', None, 'ket'), may hold values from -0.0546875 to 0.0546875
- block_values: float32 [12, 4, 4], replicated, may hold values from -3 to 3
- pair_in: int32 [12], replicated, may hold values from 0 to 3
- pair_out: int32 [12], replicated, may hold values from 0 to 3, as said below
Outputs:
- new_env: bfloat16 [4, 3072, 3072], P('mpo', 'bra', 'ket')
Inputs may be any that keep to these rules, and one draw needn't show every extreme that they name: `pair_out`: every component number 0 to 3 appears at least once.
All inputs are finite; a program needn't handle non-finite values.
Results may differ from a plain program's by a relative error of at most 0.018.
Values may be sent and summed in bfloat16 or wider, within the bound.
No kernel may reach another device: no remote copies, remote signals or barrier semaphores. Data moves between devices by JAX's collectives and lax.ppermute only.
A program may use at most 64 MiB of HBM per device.

v0:
```python
import jax
import jax.numpy as jnp
from jax import lax
from jax.sharding import Mesh
from jax.sharding import PartitionSpec as P

K = 4
BRA = ("bra_0", "bra_1")


def from_everyone(value, axis):
    copies = jnp.broadcast_to(value, (lax.axis_size(axis), *value.shape))
    return lax.all_to_all(copies, axis, split_axis=0, concat_axis=0, tiled=True)


def joined_along(blocks, dim):
    blocks = jnp.moveaxis(blocks, 0, dim)
    dims = blocks.shape
    return blocks.reshape(*dims[:dim], dims[dim] * dims[dim + 1], *dims[dim + 2 :])


def gathered_copies(value, axis, dim):
    blocks = from_everyone(value, axis)
    return joined_along(blocks, dim)


def reduced_to_own(blocks, axes, sequence):
    dims = [lax.axis_size(a) for a in axes]
    blocks = blocks.reshape(*dims, *blocks.shape[1:])
    blocks = blocks.transpose(*sequence, *range(len(axes), blocks.ndim))
    blocks = blocks.reshape(-1, *blocks.shape[len(axes) :])
    for k in sequence:
        blocks = lax.psum_scatter(blocks, axes[k], scatter_dimension=0, tiled=True)
    return blocks[0]


def cut_along(value, dim, peers):
    dims = value.shape
    blocks = value.reshape(*dims[:dim], peers, dims[dim] // peers, *dims[dim + 1 :])
    return jnp.moveaxis(blocks, dim, 0)


def scatter_axes(value, axes, sequence, dim):
    peers = lax.axis_size(axes)
    return reduced_to_own(cut_along(value, dim, peers), axes, sequence)


def local(left_env, site_tensor, block_values, pair_in, pair_out):
    comps_loc = left_env.shape[0]
    rows_loc = left_env.shape[1]
    cols_loc = left_env.shape[2]
    phys = site_tensor.shape[1]
    comps = jnp.arange(K, dtype=jnp.int32)
    hot_out = (pair_out[:, None] == comps[None, :]).astype(jnp.float32)
    hot_in = (pair_in[:, None] == comps[None, :]).astype(jnp.float32)
    mixing = jnp.einsum("pv,pw,pst->vswt", hot_out, hot_in, block_values)
    own_start = lax.axis_index("mpo") * comps_loc
    site_full = lax.all_gather(site_tensor, BRA, axis=0, tiled=True)
    full_rows = site_full.shape[0]
    site_flat = site_full.reshape(full_rows, phys * cols_loc)
    piece = gathered_copies(left_env, "ket", 2)
    width = piece.shape[2]
    panel = site_flat
    half = jnp.dot(
        piece.reshape(comps_loc * rows_loc, width), panel, preferred_element_type=jnp.float32
    )
    half = half.astype(jnp.bfloat16).reshape(comps_loc, rows_loc, phys, cols_loc)
    halves = gathered_copies(half, "mpo", 0)
    mix_rows = lax.dynamic_slice_in_dim(mixing, own_start, comps_loc, 0)
    mixed = jnp.einsum("vswt,watc->vasc", mix_rows, halves.astype(jnp.float32)).astype(jnp.bfloat16)
    site_wide = lax.all_gather(site_tensor, "ket", axis=2, tiled=True)
    site_pairs = site_wide.reshape(rows_loc * phys, site_wide.shape[2])
    mixed_pairs = mixed.reshape(comps_loc, rows_loc * phys, cols_loc)
    panel = site_pairs
    owned = scatter_axes(
        jnp.einsum("ke,wkc->ewc", panel, mixed_pairs, preferred_element_type=jnp.float32).astype(
            jnp.bfloat16
        ),
        BRA,
        (1, 0),
        0,
    ).astype(jnp.float32)
    return jnp.transpose(owned, (1, 0, 2)).astype(jnp.bfloat16)


def solution(mesh):
    finer = Mesh(
        mesh.devices.reshape(4, 4, mesh.shape["ket"], mesh.shape["mpo"]),
        ("bra_0", "bra_1", "ket", "mpo"),
    )
    return jax.shard_map(
        local,
        mesh=finer,
        in_specs=(P("mpo", BRA, "ket"), P(BRA, None, "ket"), P(), P(), P()),
        out_specs=P("mpo", BRA, "ket"),
        check_vma=False,
    )
```

profile of v0, /device:TPU:1, one launch (start us, length us, event | category | flops | bytes accessed | tf_op | source)
XLA Modules:
  0.0 318.4 jit_solution(14838852774448430552)
XLA Ops:
  6.5 0.0 copy-start
  6.5 0.0 copy-start.1
  6.5 0.0 all-gather.3.cloned.1.call-start
  6.5 0.7 all-gather.3.cloned.1.call-update
  7.3 0.0 all-gather.5.cloned.1.call-start
  7.3 1.9 copy.20
  9.3 0.0 all-gather.5.cloned.1.call-update
  9.3 0.0 copy-done.1
  9.3 0.3 broadcast_in_dim.4
  9.6 35.1 %all_to_all.10 = bf16[8,2,192,384]{3,2,1,0:T(8,128)(2,1)S(1)} all-to-all(bf16[8,2,192,384]{3,2,1,0:T(8,128)(2,1)S(1)} %broadcast_in_dim.4), channel_id=1, replica_groups=mesh['bra_0'=4,'bra_1'=4,'ket'=8,'mpo'=2] {'ket'}, dimensions={0} | all-to-all | bytes 4718592 | tf_op jit(solution)/shard_map/all_to_all | solution.py:13
  44.7 1.4 copy.16
  46.1 0.5 copy.28
  46.6 79.0 %all-gather.3.cloned.1.call-done = bf16[3072,4,384]{2,1,0:T(4,128)(2,1)} async-done(((bf16[192,4,384]{2,1,0:T(4,128)(2,1)}), bf16[3072,4,384]{2,1,0:T(4,128)(2,1)}) %all-gather.3.cloned.1.call-update) | async-done | bytes 9437200 | tf_op jit(solution)/shard_map/all_gather | solution.py:58
  125.7 9.0 %copy.29 = bf16[384,8,4,384]{3,1,2,0:T(8,128)(2,1)} copy(bf16[384,8,4,384]{3,2,1,0:T(4,128)(2,1)} %bitcast.64) | data formatting | bytes 18874368
  134.7 6.7 %convolution_convert_fusion = bf16[384,1536]{1,0:T(8,128)(2,1)S(1)} fusion(bf16[384,3072]{1,0:T(8,128)(2,1)S(1)} %bitcast.68, bf16[3072,1536]{1,0:T(8,128)(2,1)} %bitcast.65), kind=kOutput, calls=%fused_computation.3 | convolution fusion | flops 3624468480 | bytes 12976128 | tf_op jit(solution)/shard_map/dot_general | solution.py:64
  141.4 0.3 reshape.19
  141.7 0.4 copy.17
  142.1 2.0 broadcast_in_dim.5
  144.2 0.0 copy-start.2
  144.2 0.0 copy-start.3
  144.2 4.0 %all-to-all-start.1 = ((bf16[2,2,192,4,384]{4,3,1,2,0:T(4,128)(2,1)}), bf16[2,2,192,4,384]{4,3,1,2,0:T(4,128)(2,1)S(1)}, u32[]{:S(2)}, u32[]{:S(2)}) async-start(bf16[2,2,192,4,384]{4,3,1,2,0:T(4,128)(2,1)} %broadcast_in_dim.5), calls=%async_computation.1 | async-start | bytes 4718592 | tf_op jit(solution)/shard_map/all_to_all | solution.py:13
  148.2 0.0 reduce-scatter.3.cloned.1.call-start
  148.2 0.0 copy-done.2
  148.2 0.0 copy-done.3
  148.3 0.0 copy-done
  148.3 0.1 fusion.8
  148.5 39.8 %all-to-all-done.1 = bf16[2,2,192,4,384]{4,3,1,2,0:T(4,128)(2,1)S(1)} async-done(((bf16[2,2,192,4,384]{4,3,1,2,0:T(4,128)(2,1)}), bf16[2,2,192,4,384]{4,3,1,2,0:T(4,128)(2,1)S(1)}, u32[]{:S(2)}, u32[]{:S(2)}) %all-to-all-start.1) | async-done | bytes 2359328 | tf_op jit(solution)/shard_map/all_to_all | solution.py:13
  188.3 0.8 copy.18
  189.1 1.6 fusion.4
  190.7 0.0 all-gather.5.cloned.1.call-done
  190.7 7.9 %fusion.1 = bf16[3072,2,384]{0,2,1:T(8,128)(2,1)} fusion(bf16[192,4,3072]{2,0,1:T(8,128)(2,1)} %all-gather.5.cloned.1.call-done, bf16[2,192,4,384]{3,2,0,1:T(4,128)(2,1)S(1)} %fusion.4), kind=kOutput, calls=%fused_computation.2 | convolution fusion | flops 3626237952 | bytes 10616832 | tf_op jit(solution)/shard_map/ke,wkc->ewc/dot_general | solution.py:76
  198.6 6.7 %copy.22 = bf16[3072,2,384]{2,0,1:T(8,128)(2,1)} copy(bf16[3072,2,384]{0,2,1:T(8,128)(2,1)} %fusion.1) | data formatting | bytes 9437184 | tf_op jit(solution)/shard_map/convert_element_type | solution.py:76
  205.3 5.1 %copy.23 = bf16[4,4,192,2,384]{4,2,3,1,0:T(8,128)(2,1)} copy(bf16[4,4,192,2,384]{4,2,0,1,3:T(8,128)(2,1)} %bitcast.63) | data formatting | bytes 9437184 | tf_op jit(solution)/shard_map/transpose | solution.py:30
  210.3 0.0 reduce-scatter.3.cloned.1.call-update
  210.4 0.0 reduce-scatter.5.cloned.1.call-start
  210.4 65.0 %reduce-scatter.3.cloned.1.call-done = bf16[4,192,2,384]{3,1,2,0:T(8,128)(2,1)} async-done(((bf16[16,192,2,384]{3,1,2,0:T(8,128)(2,1)}), bf16[4,192,2,384]{3,1,2,0:T(8,128)(2,1)}) %reduce-scatter.3.cloned.1.call-update) | async-done | bytes 1179664 | tf_op jit(solution)/shard_map/reduce_scatter | solution.py:33
  275.4 0.0 reduce-scatter.5.cloned.1.call-update
  275.4 36.5 %reduce-scatter.5.cloned.1.call-done = bf16[1,192,2,384]{3,1,2,0:T(8,128)(2,1)} async-done(((bf16[4,192,2,384]{3,1,2,0:T(8,128)(2,1)}), bf16[1,192,2,384]{3,1,2,0:T(8,128)(2,1)}) %reduce-scatter.5.cloned.1.call-update) | async-done | bytes 294928 | tf_op jit(solution)/shard_map/reduce_scatter | solution.py:33
  (2 shorter events, 0.0 us)
Async XLA Ops:
  6.5 141.7 %copy-start = (f32[12,4,4]{0,2,1:T(4,128)S(1)}, f32[12,4,4]{0,2,1:T(4,128)}, u32[]{:S(2)}) copy-start(f32[12,4,4]{0,2,1:T(4,128)} %param.7) | copy-start | bytes 2308
  6.5 2.7 copy-start.1
  6.5 119.1 %all-gather.3.cloned.1.call-start = ((), (), s32[]{:S(2)}) async-start(), calls=%async_computation.4 | async-start | bytes 10027008 | tf_op jit(solution)/shard_map/all_gather | solution.py:58
  7.3 183.4 %all-gather.5.cloned.1.call-start = ((), (), s32[]{:S(2)}) async-start(), calls=%async_computation.5 | async-start | bytes 5308416 | tf_op jit(solution)/shard_map/all_gather | solution.py:71
  144.2 4.1 %copy-start.2 = (s32[12]{0:T(128)S(1)}, s32[12]{0:T(128)}, u32[]{:S(2)}) copy-start(s32[12]{0:T(128)} %param.8) | copy-start | bytes 148
  144.2 4.1 %copy-start.3 = (s32[12]{0:T(128)S(1)}, s32[12]{0:T(128)}, u32[]{:S(2)}) copy-start(s32[12]{0:T(128)} %param.9) | copy-start | bytes 148
  144.2 44.1 %all-to-all-start.1 = ((bf16[2,2,192,4,384]{4,3,1,2,0:T(4,128)(2,1)}), bf16[2,2,192,4,384]{4,3,1,2,0:T(4,128)(2,1)S(1)}, u32[]{:S(2)}, u32[]{:S(2)}) async-start(bf16[2,2,192,4,384]{4,3,1,2,0:T(4,128)(2,1)} %broadcast_in_dim.5), calls=%async_computation.1 | async-start | bytes 4718592 | tf_op jit(solution)/shard_map/all_to_all | solution.py:13
  148.2 127.2 %reduce-scatter.3.cloned.1.call-start = ((), (), s32[]{:S(2)}) async-start(), calls=%async_computation.6 | async-start | bytes 5898240 | tf_op jit(solution)/shard_map/reduce_scatter | solution.py:33
  210.4 101.5 %reduce-scatter.5.cloned.1.call-start = ((), (), s32[]{:S(2)}) async-start(), calls=%async_computation.7 | async-start | bytes 1474560 | tf_op jit(solution)/shard_map/reduce_scatter | solution.py:33
Sparse Core Ops, SparseCore 0:
  9.1 116.5 all-gather.2
  127.5 34.0 all-gather.4
  210.5 64.8 reduce-scatter.2
  277.8 34.0 reduce-scatter.4
where the time goes:
time: 319 us; the launch traced here: 318 us
  waiting for transfers between devices  221 us (69%)
  blocking collectives  35.1 us (11%)
  local copies, waits for them, and re-layouts  28.5 us (9%)
  matrix products  16.3 us (5%)
  between operations  13.3 us (4%)
  starting transfers between devices  4.12 us (1%)
    reduce_scatter x2, waiting for transfers between devices, reduced_to_own(): blocks = lax.psum_scatter(blocks, axes[k], scatter_dimension=0, tiled=True)  101 us
    all_gather x1, waiting for transfers between devices, local(): site_full = lax.all_gather(site_tensor, BRA, axis=0, tiled=True)  79 us
    all_to_all x1, waiting for transfers between devices, from_everyone(): return lax.all_to_all(copies, axis, split_axis=0, concat_axis=0, tiled=True)  39.8 us
    all_to_all x1, blocking collectives, from_everyone(): return lax.all_to_all(copies, axis, split_axis=0, concat_axis=0, tiled=True)  35.1 us
    unnamed x11, local copies, waits for them, and re-layouts  11.4 us
    dot_general x1, matrix products, local(): jnp.einsum('ke,wkc->ewc', panel, mixed_pairs, preferred_element_type=jnp....  7.87 us
    dot_general x1, matrix products, local(): jnp.dot(piece.reshape(comps_loc * rows_loc, width), panel, preferred_elem...  6.74 us
    convert_element_type x1, local copies, waits for them, and re-layouts, local(): jnp.einsum('ke,wkc->ewc', panel, mixed_pairs, preferred_element_type=jnp....  6.73 us
  transfers between devices with their start and end apart: 5, of which 4 were waited for; matrix products, arithmetic and copies ran while one was open for 8% of the time, Pallas kernels for 0%

commit v1 on v0

--- a/solution.py
+++ b/solution.py
@@ -6,6 +6,13 @@
 
 K = 4
 BRA = ("bra_0", "bra_1")
+
+
+def gather_over(x, name, d):
+    peers = lax.axis_size(name)
+    pieces = jnp.stack([x for _ in range(peers)])
+    pieces = lax.all_to_all(pieces, name, split_axis=0, concat_axis=0)
+    return jnp.concatenate(pieces, axis=d)
 
 
 def from_everyone(value, axis):
@@ -55,7 +62,7 @@
     hot_in = (pair_in[:, None] == comps[None, :]).astype(jnp.float32)
     mixing = jnp.einsum("pv,pw,pst->vswt", hot_out, hot_in, block_values)
     own_start = lax.axis_index("mpo") * comps_loc
-    site_full = lax.all_gather(site_tensor, BRA, axis=0, tiled=True)
+    site_full = gather_over(site_tensor, BRA, 0)
     full_rows = site_full.shape[0]
     site_flat = site_full.reshape(full_rows, phys * cols_loc)
     piece = gathered_copies(left_env, "ket", 2)

time: 319 us -> 461 us (1.45)
  waiting for transfers between devices: 221 us -> 347 us
  starting transfers between devices: 4.12 us -> 13.9 us
  local copies, waits for them, and re-layouts: 28.5 us -> 35.7 us
    all_to_all x0 -> x1, waiting for transfers between devices: none -> 167 us  [gather_over(): pieces = lax.all_to_all(pieces, name, split_axis=0, concat_axis=0)]
    all_gather x1 -> x0, waiting for transfers between devices: 79 us -> none  [local(): site_full = lax.all_gather(site_tensor, BRA, axis=0, tiled=True)]
    reduce_scatter x2, waiting for transfers between devices: 101 us -> 151 us  [reduced_to_own(): blocks = lax.psum_scatter(blocks, axes[k], scatter_dimension=0, tiled=True)]
    all_to_all x1, waiting for transfers between devices: 39.8 us -> 28.8 us  [from_everyone(): return lax.all_to_all(copies, axis, split_axis=0, concat_axis=0, tiled=True)]
    all_to_all x0 -> x1, starting transfers between devices: none -> 8.23 us  [gather_over(): pieces = lax.all_to_all(pieces, name, split_axis=0, concat_axis=0)]
    another operation x0 -> x1, local copies, waits for them, and re-layouts: none -> 7.29 us  [gather_over(): pieces = jnp.stack([x for _ in range(peers)])]
  transfers between devices with their start and end apart: 5 -> 5, of which waited for: 4 -> 4; matrix products, arithmetic and copies ran while one was open for 8% -> 5% of each run, Pallas kernels for 0% -> 0%
where the time goes in v1:
time: 461 us; the launch traced here: 460 us
  waiting for transfers between devices  347 us (75%)
  local copies, waits for them, and re-layouts  35.7 us (8%)
  blocking collectives  34.9 us (8%)
  matrix products  16 us (3%)
  starting transfers between devices  13.9 us (3%)
  between operations  13.2 us (3%)
    all_to_all x1, waiting for transfers between devices, gather_over(): pieces = lax.all_to_all(pieces, name, split_axis=0, concat_axis=0)  167 us
    reduce_scatter x2, waiting for transfers between devices, reduced_to_own(): blocks = lax.psum_scatter(blocks, axes[k], scatter_dimension=0, tiled=True)  151 us
    all_to_all x1, blocking collectives, from_everyone(): return lax.all_to_all(copies, axis, split_axis=0, concat_axis=0, tiled=True)  34.9 us
    all_to_all x1, waiting for transfers between devices, from_everyone(): return lax.all_to_all(copies, axis, split_axis=0, concat_axis=0, tiled=True)  28.8 us
    unnamed x11, local copies, waits for them, and re-layouts  10.4 us
  transfers between devices with their start and end apart: 5, of which 4 were waited for; matrix products, arithmetic and copies ran while one was open for 5% of the time, Pallas kernels for 0%

profile of v1, /device:TPU:1, one launch (start us, length us, event | category | flops | bytes accessed | tf_op | source)
XLA Modules:
  0.0 460.3 jit_solution(12973855476002474575)
XLA Ops:
  6.5 0.0 copy-start
  6.5 1.3 broadcast_in_dim.4
  7.8 0.0 copy-start.1
  7.8 34.9 %all_to_all.15 = bf16[8,2,192,384]{3,2,1,0:T(8,128)(2,1)S(1)} all-to-all(bf16[8,2,192,384]{3,2,1,0:T(8,128)(2,1)S(1)} %broadcast_in_dim.4), channel_id=1, replica_groups=mesh['bra_0'=4,'bra_1'=4,'ket'=8,'mpo'=2] {'ket'}, dimensions={0} | all-to-all | bytes 4718592 | tf_op jit(solution)/shard_map/all_to_all | solution.py:20
  42.7 0.0 copy-done.1
  42.7 7.3 %stack.2 = bf16[16,192,4,384]{3,2,1,0:T(4,128)(2,1)} broadcast(bf16[192,4,384]{2,1,0:T(4,128)(2,1)S(1)} %copy-done.1), dimensions={1,2,3} | broadcast | bytes 10027008 | tf_op jit(solution)/shard_map/stack | solution.py:13
  50.0 8.2 %all-to-all-start.1 = ((bf16[16,192,4,384]{3,2,1,0:T(4,128)(2,1)}), bf16[16,192,4,384]{3,2,1,0:T(4,128)(2,1)}, u32[]{:S(2)}, u32[]{:S(2)}) async-start(bf16[16,192,4,384]{3,2,1,0:T(4,128)(2,1)} %stack.2), calls=%async_computation.1 | async-start | bytes 18874368 | tf_op jit(solution)/shard_map/all_to_all | solution.py:14
  58.2 0.0 all-gather.2.cloned.1.call-start
  58.3 0.9 copy.20
  59.2 0.0 all-gather.2.cloned.1.call-update
  59.2 1.4 copy.16
  60.6 0.5 copy.28
  61.1 166.7 %all-to-all-done.1 = bf16[16,192,4,384]{3,2,1,0:T(4,128)(2,1)} async-done(((bf16[16,192,4,384]{3,2,1,0:T(4,128)(2,1)}), bf16[16,192,4,384]{3,2,1,0:T(4,128)(2,1)}, u32[]{:S(2)}, u32[]{:S(2)}) %all-to-all-start.1) | async-done | bytes 9437216 | tf_op jit(solution)/shard_map/all_to_all | solution.py:14
  227.8 9.0 %copy.29 = bf16[384,8,4,384]{3,1,2,0:T(8,128)(2,1)} copy(bf16[384,8,4,384]{3,2,1,0:T(4,128)(2,1)} %bitcast.30) | data formatting | bytes 18874368
  236.8 6.5 %convolution_convert_fusion = bf16[384,1536]{1,0:T(8,128)(2,1)S(1)} fusion(bf16[384,3072]{1,0:T(8,128)(2,1)S(1)} %bitcast.68, bf16[3072,1536]{1,0:T(8,128)(2,1)} %bitcast.65), kind=kOutput, calls=%fused_computation.3 | convolution fusion | flops 3624468480 | bytes 12976128 | tf_op jit(solution)/shard_map/dot_general | solution.py:71
  243.3 0.3 reshape.17
  243.6 0.4 copy.17
  244.0 2.0 broadcast_in_dim.5
  246.0 0.0 copy-start.2
  246.0 0.0 copy-start.3
  246.0 5.6 %all-to-all-start.2 = ((bf16[2,2,192,4,384]{4,3,1,2,0:T(4,128)(2,1)}), bf16[2,2,192,4,384]{4,3,1,2,0:T(4,128)(2,1)S(1)}, u32[]{:S(2)}, u32[]{:S(2)}) async-start(bf16[2,2,192,4,384]{4,3,1,2,0:T(4,128)(2,1)} %broadcast_in_dim.5), calls=%async_computation.2 | async-start | bytes 4718592 | tf_op jit(solution)/shard_map/all_to_all | solution.py:20
  251.6 0.0 reduce-scatter.3.cloned.1.call-start
  251.6 0.0 copy-done.2
  251.6 0.0 copy-done.3
  251.6 0.0 copy-done
  251.6 0.1 fusion.8
  251.8 28.8 %all-to-all-done.2 = bf16[2,2,192,4,384]{4,3,1,2,0:T(4,128)(2,1)S(1)} async-done(((bf16[2,2,192,4,384]{4,3,1,2,0:T(4,128)(2,1)}), bf16[2,2,192,4,384]{4,3,1,2,0:T(4,128)(2,1)S(1)}, u32[]{:S(2)}, u32[]{:S(2)}) %all-to-all-start.2) | async-done | bytes 2359328 | tf_op jit(solution)/shard_map/all_to_all | solution.py:20
  280.6 0.8 copy.18
  281.4 1.6 fusion.4
  283.0 0.0 all-gather.2.cloned.1.call-done
  283.0 7.9 %fusion.1 = bf16[3072,2,384]{0,2,1:T(8,128)(2,1)} fusion(bf16[192,4,3072]{2,0,1:T(8,128)(2,1)} %all-gather.2.cloned.1.call-done, bf16[2,192,4,384]{3,2,0,1:T(4,128)(2,1)S(1)} %fusion.4), kind=kOutput, calls=%fused_computation.2 | convolution fusion | flops 3626237952 | bytes 10616832 | tf_op jit(solution)/shard_map/ke,wkc->ewc/dot_general | solution.py:83
  290.9 6.7 %copy.22 = bf16[3072,2,384]{2,0,1:T(8,128)(2,1)} copy(bf16[3072,2,384]{0,2,1:T(8,128)(2,1)} %fusion.1) | data formatting | bytes 9437184 | tf_op jit(solution)/shard_map/convert_element_type | solution.py:83
  297.6 5.1 %copy.23 = bf16[4,4,192,2,384]{4,2,3,1,0:T(8,128)(2,1)} copy(bf16[4,4,192,2,384]{4,2,0,1,3:T(8,128)(2,1)} %bitcast.64) | data formatting | bytes 9437184 | tf_op jit(solution)/shard_map/transpose | solution.py:37
  302.6 0.0 reduce-scatter.3.cloned.1.call-update
  302.7 0.0 reduce-scatter.5.cloned.1.call-start
  302.7 114.4 %reduce-scatter.3.cloned.1.call-done = bf16[4,192,2,384]{3,1,2,0:T(8,128)(2,1)} async-done(((bf16[16,192,2,384]{3,1,2,0:T(8,128)(2,1)}), bf16[4,192,2,384]{3,1,2,0:T(8,128)(2,1)}) %reduce-scatter.3.cloned.1.call-update) | async-done | bytes 1179664 | tf_op jit(solution)/shard_map/reduce_scatter | solution.py:40
  417.1 0.0 reduce-scatter.5.cloned.1.call-update
  417.2 36.6 %reduce-scatter.5.cloned.1.call-done = bf16[1,192,2,384]{3,1,2,0:T(8,128)(2,1)} async-done(((bf16[4,192,2,384]{3,1,2,0:T(8,128)(2,1)}), bf16[1,192,2,384]{3,1,2,0:T(8,128)(2,1)}) %reduce-scatter.5.cloned.1.call-update) | async-done | bytes 294928 | tf_op jit(solution)/shard_map/reduce_scatter | solution.py:40
  (2 shorter events, 0.0 us)
Async XLA Ops:
  6.5 245.1 %copy-start = (f32[12,4,4]{0,2,1:T(4,128)S(1)}, f32[12,4,4]{0,2,1:T(4,128)}, u32[]{:S(2)}) copy-start(f32[12,4,4]{0,2,1:T(4,128)} %param.7) | copy-start | bytes 2308
  7.8 34.9 %copy-start.1 = (bf16[192,4,384]{2,1,0:T(4,128)(2,1)S(1)}, bf16[192,4,384]{2,1,0:T(4,128)(2,1)}, u32[]{:S(2)}) copy-start(bf16[192,4,384]{2,1,0:T(4,128)(2,1)} %param.6) | copy-start | bytes 1769476
  50.0 177.8 %all-to-all-start.1 = ((bf16[16,192,4,384]{3,2,1,0:T(4,128)(2,1)}), bf16[16,192,4,384]{3,2,1,0:T(4,128)(2,1)}, u32[]{:S(2)}, u32[]{:S(2)}) async-start(bf16[16,192,4,384]{3,2,1,0:T(4,128)(2,1)} %stack.2), calls=%async_computation.1 | async-start | bytes 18874368 | tf_op jit(solution)/shard_map/all_to_all | solution.py:14
  58.2 224.8 %all-gather.2.cloned.1.call-start = ((), (), s32[]{:S(2)}) async-start(), calls=%async_computation.5 | async-start | bytes 5308416 | tf_op jit(solution)/shard_map/all_gather | solution.py:78
  246.0 5.6 %copy-start.2 = (s32[12]{0:T(128)S(1)}, s32[12]{0:T(128)}, u32[]{:S(2)}) copy-start(s32[12]{0:T(128)} %param.8) | copy-start | bytes 148
  246.0 5.6 %copy-start.3 = (s32[12]{0:T(128)S(1)}, s32[12]{0:T(128)}, u32[]{:S(2)}) copy-start(s32[12]{0:T(128)} %param.9) | copy-start | bytes 148
  246.0 34.6 %all-to-all-start.2 = ((bf16[2,2,192,4,384]{4,3,1,2,0:T(4,128)(2,1)}), bf16[2,2,192,4,384]{4,3,1,2,0:T(4,128)(2,1)S(1)}, u32[]{:S(2)}, u32[]{:S(2)}) async-start(bf16[2,2,192,4,384]{4,3,1,2,0:T(4,128)(2,1)} %broadcast_in_dim.5), calls=%async_computation.2 | async-start | bytes 4718592 | tf_op jit(solution)/shard_map/all_to_all | solution.py:20
  251.6 165.6 %reduce-scatter.3.cloned.1.call-start = ((), (), s32[]{:S(2)}) async-start(), calls=%async_computation.6 | async-start | bytes 5898240 | tf_op jit(solution)/shard_map/reduce_scatter | solution.py:40
  302.7 151.1 %reduce-scatter.5.cloned.1.call-start = ((), (), s32[]{:S(2)}) async-start(), calls=%async_computation.7 | async-start | bytes 1474560 | tf_op jit(solution)/shard_map/reduce_scatter | solution.py:40
Sparse Core Ops, SparseCore 0:
  60.9 36.3 all-gather.1
  302.8 114.3 reduce-scatter.2
  419.7 34.0 reduce-scatter.4
